TPU v7x, 32 devices: a whole 2x2x4 slice. The times are simulated.
32 devices in a mesh: aa: 8 (over y, x, core), ba: 4 (over z).
Axes of the slice: x: 2, y: 2, z: 4, core: 2. Of those that a mesh axis runs over, the one named last changes fastest.
Arguments:
- query: bfloat16 [3072, 4096], P('aa', 'ba'), may hold values from -28 to 28
- keys: bfloat16 [3072, 2048], P('aa', 'ba'), may hold values from -6 to 6
- values: bfloat16 [3072, 2048], P('aa', 'ba'), may hold values from -6 to 6
- grad_out: bfloat16 [3072, 5376], P('aa', 'ba'), may hold values from -6 to 6
- segment_ids: int32 [3072], P('aa'), may hold values from 0 to 5, never falling along the last dimension, each value on 1 to 1920 neighbouring positions
- w_query: bfloat16 [5376, 4096], P(None, 'ba'), may hold values from -0.125 to 0.125
- w_key: bfloat16 [5376, 2048], P(None, 'ba'), may hold values from -0.1875 to 0.1875
- w_value: bfloat16 [5376, 2048], P(None, 'ba'), may hold values from -0.1875 to 0.1875
- w_out: bfloat16 [4096, 5376], P('ba'), may hold values from -0.078125 to 0.078125
Outputs:
- grad_input: bfloat16 [3072, 5376], P('aa', 'ba')
Inputs may be any that keep to these rules, and one draw needn't show every extreme that they name: `segment_ids`: never falls along the sequence; each document has at most 1920 positions.
All inputs are finite; a program needn't handle non-finite values.
Results may differ from a plain program's by a relative error of at most 0.019.
Values may be sent and summed in bfloat16 or wider, within the bound.
A program may use at most 128 MiB of HBM per device.

v0:
```python
import jax
import jax.numpy as jnp
from jax import lax
from jax.sharding import PartitionSpec as P

D = 5376
HQ = 32
HD = 128


NEG_FILL = -1e30


def from_behind(value, axis, steps):
    count = lax.axis_size(axis)
    pairs = [(source, (source + steps) % count) for source in range(count)]
    return lax.ppermute(value, axis, pairs)


def block_scores(query, dout, keys, values, query_pos, query_seg, key_pos, key_seg, scaling):
    row_count = query.shape[0]
    col_count = keys.shape[0]
    groups = keys.shape[1] // HD
    query_four = query.reshape(row_count, groups, 2, HD)
    dout_four = dout.reshape(row_count, groups, 2, HD)
    key_three = keys.reshape(col_count, groups, HD)
    value_three = values.reshape(col_count, groups, HD)
    scores = (
        jnp.einsum("iagd,jad->agij", query_four, key_three, preferred_element_type=jnp.float32)
        * scaling
    )
    dprobs = jnp.einsum(
        "iagd,jad->agij", dout_four, value_three, preferred_element_type=jnp.float32
    )
    allowed = (key_pos[None, :] <= query_pos[:, None]) & (key_seg[None, :] == query_seg[:, None])
    return (scores, dprobs, allowed, query_four, dout_four, key_three)


def forward_stats(
    query, dout, keys, values, query_pos, query_seg, key_pos, key_seg, scaling, state
):
    run_max, run_sum, run_dot = state
    scores, dprobs, allowed, unused_q, unused_d, unused_k = block_scores(
        query, dout, keys, values, query_pos, query_seg, key_pos, key_seg, scaling
    )
    masked = jnp.where(allowed, scores, NEG_FILL)
    new_max = jnp.maximum(run_max, jnp.max(masked, axis=-1))
    expo = jnp.where(allowed, jnp.exp(scores - new_max[..., None]), 0.0)
    return (new_max, jnp.sum(expo, axis=-1), jnp.sum(expo * dprobs, axis=-1))


def block_grads(
    query, dout, row_lse, row_delta, keys, values, query_pos, query_seg, key_pos, key_seg, scaling
):
    scores, dprobs, allowed, query_four, dout_four, key_three = block_scores(
        query, dout, keys, values, query_pos, query_seg, key_pos, key_seg, scaling
    )
    softmax_w = jnp.where(allowed, jnp.exp(scores - row_lse[..., None]), 0.0)
    dscores = softmax_w * (dprobs - row_delta[..., None])
    softmax_low = softmax_w.astype(jnp.bfloat16)
    dscores_low = dscores.astype(jnp.bfloat16)
    grad_v = jnp.einsum(
        "agij,iagd->jad", softmax_low, dout_four, preferred_element_type=jnp.float32
    )
    grad_k = (
        jnp.einsum("agij,iagd->jad", dscores_low, query_four, preferred_element_type=jnp.float32)
        * scaling
    )
    grad_q = (
        jnp.einsum("agij,jad->iagd", dscores_low, key_three, preferred_element_type=jnp.float32)
        * scaling
    )
    return (
        grad_q.reshape(query.shape[0], -1),
        grad_k.reshape(keys.shape[0], -1),
        grad_v.reshape(keys.shape[0], -1),
    )


def project_back(grad, weight):
    return lax.dot_general(
        grad, weight, (((1,), (1,)), ((), ())), preferred_element_type=jnp.float32
    )


def local(query, keys, values, grad_out, segment_ids, w_query, w_key, w_value, w_out):
    seq_devices = lax.axis_size("aa")
    own_index = lax.axis_index("aa")
    tok_count = query.shape[0]
    scaling = (D / HQ) ** (-0.5)
    groups = keys.shape[1] // HD
    all_seg = lax.all_gather(segment_ids, "aa", axis=0, tiled=True)
    dout = project_back(lax.all_gather(grad_out, "ba", axis=1, tiled=True), w_out).astype(
        jnp.bfloat16
    )
    offsets = lax.iota(jnp.int32, tok_count)
    own_pos = own_index * tok_count + offsets
    own_seg = lax.dynamic_slice_in_dim(all_seg, own_index * tok_count, tok_count)
    stat_shape = (groups, 2, tok_count)
    stats_start = (
        jnp.full(stat_shape, NEG_FILL, jnp.float32),
        jnp.zeros(stat_shape, jnp.float32),
        jnp.zeros(stat_shape, jnp.float32),
    )
    piece = (
        lax.all_gather(keys, "aa", axis=0, tiled=True),
        lax.all_gather(values, "aa", axis=0, tiled=True),
    )
    width = piece[0].shape[0]
    key_pos = lax.iota(jnp.int32, width)
    key_seg = all_seg
    run_max, run_sum, run_dot = forward_stats(
        query, dout, piece[0], piece[1], own_pos, own_seg, key_pos, key_seg, scaling, stats_start
    )
    row_lse = run_max + jnp.log(run_sum)
    row_delta = run_dot / run_sum
    zero_q = jnp.zeros(query.shape, jnp.float32)
    zero_k = jnp.zeros(keys.shape, jnp.float32)

    def step_keys(step_index, state):
        (keys_now, values_now), (dk_now, dv_now), grad_q = state
        anchor = (own_index - step_index) % seq_devices
        key_pos = anchor * tok_count + offsets
        key_seg = lax.dynamic_slice_in_dim(all_seg, anchor * tok_count, tok_count)
        add_q, add_k, add_v = block_grads(
            query,
            dout,
            row_lse,
            row_delta,
            keys_now,
            values_now,
            own_pos,
            own_seg,
            key_pos,
            key_seg,
            scaling,
        )
        bundle_next = from_behind((keys_now, values_now), "aa", 1)
        sums_next = (
            from_behind((dk_now + add_k).astype(jnp.bfloat16), "aa", 1).astype(jnp.float32),
            from_behind((dv_now + add_v).astype(jnp.bfloat16), "aa", 1).astype(jnp.float32),
        )
        return (bundle_next, sums_next, grad_q + add_q)

    initial = ((keys, values), (zero_k, zero_k), zero_q)
    final = lax.fori_loop(0, seq_devices, step_keys, initial)
    grad_q = final[2]
    grad_k = final[1][0]
    grad_v = final[1][1]
    partial_value = (
        project_back(grad_q.astype(jnp.bfloat16), w_query)
        + project_back(grad_k.astype(jnp.bfloat16), w_key)
        + project_back(grad_v.astype(jnp.bfloat16), w_value)
    )
    return lax.psum_scatter(
        partial_value.astype(jnp.bfloat16), "ba", scatter_dimension=1, tiled=True
    )


def solution(mesh):
    return jax.shard_map(
        local,
        mesh=mesh,
        in_specs=(
            P("aa", "ba"),
            P("aa", "ba"),
            P("aa", "ba"),
            P("aa", "ba"),
            P("aa"),
            P(None, "ba"),
            P(None, "ba"),
            P(None, "ba"),
            P("ba", None),
        ),
        out_specs=P("aa", "ba"),
        check_vma=False,
    )
```

profile of v0, /device:TPU:0, one launch (start us, length us, event | category | flops | bytes accessed | tf_op | source)
XLA Modules:
  0.0 465.6 jit_solution(3286904007200028266)
XLA Ops:
  7.6 1.9 copy.54
  12.9 10.4 %all-gather = s32[8,1,384]{2,1,0:T(1,128)S(1)} all-gather(s32[1,1,384]{2,1,0:T(1,128)S(1)} %reshape.106), channel_id=1, replica_groups=mesh['aa'=8,'ba'=4] {'aa'}, dimensions={0}, use_global_device_ids=true | all-gather | bytes 13824 | tf_op jit(solution)/shard_map/all_gather | solution.py:92
  23.4 2.9 fusion.27
  26.3 18.9 %all-gather.5.cloned.1.call-done = bf16[3072,512]{0,1:T(8,128)(2,1)} async-done(((bf16[384,512]{0,1:T(8,128)(2,1)}), bf16[3072,512]{0,1:T(8,128)(2,1)}) %all-gather.5.cloned.1.call-update) | async-done | bytes 3145744 | tf_op jit(solution)/shard_map/all_gather | solution.py:106
  45.2 17.3 %fusion.22 = (f32[4,2,384]{2,1,0:T(2,128)S(1)}, f32[4,3072,384,2]{2,1,3,0:T(8,128)}) fusion(pred[384,3072]{0,1:T(8,128)(4,1)} %fusion.27, bf16[3072,4,128,1]{0,2,3,1:T(8,128)(2,1)} %bitcast.143, bf16[384,4,2,128]{3,2,1,0:T(2,128)(2,1)S(1)} %reshape.103), kind=kOutput, calls=%fused_computation.32 | convolution fusion | flops 2444227584 | bytes 42872832 | tf_op jit(solution)/shard_map/iagd,jad->agij/dot_general | solution.py:29
  63.7 16.8 %fusion.25 = f32[4,2,384]{2,1,0:T(2,128)} fusion(f32[4,3072,384,2]{2,1,3,0:T(8,128)} %get-tuple-element.486, f32[4,2,384]{2,1,0:T(2,128)S(1)} %broadcast_maximum_fusion, pred[384,3072]{0,1:T(8,128)(4,1)S(1)} %copy-done.1), kind=kLoop, calls=%fused_computation.35 | loop fusion | flops 37745664 | bytes 38952960 | tf_op jit(solution)/shard_map/reduce_sum | solution.py:49
  80.5 45.9 %all-gather.7.cloned.1.call-done = bf16[384,5376]{0,1:T(8,128)(2,1)} async-done(((bf16[384,1344]{0,1:T(8,128)(2,1)}), bf16[384,5376]{0,1:T(8,128)(2,1)}) %all-gather.7.cloned.1.call-update) | async-done | bytes 4128784 | tf_op jit(solution)/shard_map/all_gather | solution.py:93
  126.4 9.9 %convolution_convert_fusion = bf16[384,1024]{1,0:T(8,128)(2,1)S(1)} fusion(bf16[384,5376]{0,1:T(8,128)(2,1)} %all-gather.7.cloned.1.call-done, bf16[1024,5376]{1,0:T(8,128)(2,1)} %param.19), kind=kOutput, calls=%fused_computation.41 | convolution fusion | flops 4228251648 | bytes 15925248 | tf_op jit(solution)/shard_map/dot_general | solution.py:81
  138.9 20.7 %all-gather.9.cloned.1.call-done = bf16[3072,512]{0,1:T(8,128)(2,1)} async-done(((bf16[384,512]{0,1:T(8,128)(2,1)}), bf16[3072,512]{0,1:T(8,128)(2,1)}) %all-gather.9.cloned.1.call-update) | async-done | bytes 3145744 | tf_op jit(solution)/shard_map/all_gather | solution.py:107
  159.5 17.9 %fusion.21 = f32[4,2,384]{2,1,0:T(2,128)S(1)} fusion(f32[4,3072,384,2]{2,1,3,0:T(8,128)} %get-tuple-element.486, f32[4,2,384]{2,1,0:T(2,128)} %copy-done.6, pred[384,3072]{0,1:T(8,128)(4,1)} %fusion.27, bf16[3072,4,128,1]{0,2,3,1:T(8,128)(2,1)} %bitcast.144, bf16[384,4,2,128]{3,2,1,0:T(2,128)(2,1)} %reshape.104), kind=kOutput, calls=%fused_computation.29 | convolution fusion | flops 2463101952 | bytes 42885120 | tf_op jit(solution)/shard_map/iagd,jad->agij/dot_general | solution.py:32
  178.2 183.6 %while.24 = (s32[]{:T(128)}, bf16[384,512]{0,1:T(8,128)(2,1)}, bf16[384,512]{1,0:T(8,128)(2,1)S(1)}, f32[384,512]{0,1:T(8,128)S(1)}, f32[384,512]{0,1:T(8,128)S(...) while((s32[]{:T(128)}, bf16[384,512]{0,1:T(8,128)(2,1)}, ...), condition=%wide.region_4.5_spmd.clone, body=%wide.region_3.4_spmd.clone.sunk | while | flops 1525138176 | bytes 53772984 | solution.py:146
  191.8 4.1 collective-permute-done.2
  196.9 3.2 collective-permute-done.3
  210.8 1.9 collective-permute-start.3
  213.3 2.9 bitcast_add_fusion.4
  216.1 2.6 collective-permute-done.2
  219.8 3.2 collective-permute-done.3
  233.0 2.6 collective-permute-start.3
  236.2 2.9 bitcast_add_fusion.4
  239.1 2.6 collective-permute-done.2
  242.8 3.2 collective-permute-done.3
  251.0 1.5 fusion.79
  256.0 2.6 collective-permute-start.3
  259.1 2.9 bitcast_add_fusion.4
  262.0 2.7 collective-permute-done.2
  265.7 3.2 collective-permute-done.3
  278.9 2.6 collective-permute-start.3
  282.1 2.9 bitcast_add_fusion.4
  285.0 2.6 collective-permute-done.2
  288.7 3.2 collective-permute-done.3
  296.9 1.5 fusion.79
  301.9 2.6 collective-permute-start.3
  305.0 2.9 bitcast_add_fusion.4
  307.9 2.6 collective-permute-done.2
  311.6 3.2 collective-permute-done.3
  324.8 2.6 collective-permute-start.3
  328.0 2.9 bitcast_add_fusion.4
  330.9 2.7 collective-permute-done.2
  334.6 3.2 collective-permute-done.3
  342.8 1.5 fusion.79
  347.8 2.6 collective-permute-start.3
  350.9 2.9 bitcast_add_fusion.4
  353.8 2.6 collective-permute-done.2
  357.5 3.2 collective-permute-done.3
  361.8 9.3 %fusion.31 = f32[384,5376]{0,1:T(8,128)S(1)} fusion(bf16[5376,1024]{1,0:T(8,128)(2,1)} %param.16, f32[384,1024]{0,1:T(8,128)} %get-tuple-element.360), kind=kOutput, calls=%fused_computation.45 | convolution fusion | flops 4228251648 | bytes 20840448 | tf_op jit(solution)/shard_map/dot_general | solution.py:81
  371.1 5.0 %convolution_add_fusion.1 = f32[384,5376]{0,1:T(8,128)S(1)} fusion(f32[384,5376]{0,1:T(8,128)S(1)} %fusion.31, bf16[5376,512]{1,0:T(8,128)(2,1)} %param.17, f32[384,512]{0,1:T(8,128)S(1)} %get-tuple-element.361), kind=kOutput, calls=%fused_computation.37 | convolution fusion | flops 2116190208 | bytes 22806528 | tf_op jit(solution)/shard_map/dot_general | solution.py:81
  376.1 7.5 %fusion.26 = bf16[384,5376]{0,1:T(8,128)(2,1)} fusion(f32[384,5376]{0,1:T(8,128)S(1)} %convolution_add_fusion.1, bf16[5376,512]{1,0:T(8,128)(2,1)} %param.18, f32[384,512]{0,1:T(8,128)S(1)} %get-tuple-element.362), kind=kOutput, calls=%fused_computation.38 | convolution fusion | flops 2118254592 | bytes 18677760 | tf_op jit(solution)/shard_map/dot_general | solution.py:81
  383.7 75.3 %reduce-scatter.2.cloned.1.call-done = bf16[384,1344]{0,1:T(8,128)(2,1)} async-done(((bf16[384,5376]{0,1:T(8,128)(2,1)}), bf16[384,1344]{0,1:T(8,128)(2,1)}) %reduce-scatter.2.cloned.1.call-update) | async-done | bytes 1032208 | tf_op jit(solution)/shard_map/reduce_scatter | solution.py:155
  (299 shorter events, 101.2 us)
Async XLA Ops:
  6.5 6.4 %copy-start.12 = (s32[384]{0:T(512)S(1)}, s32[384]{0:T(512)}, u32[]{:S(2)}) copy-start(s32[384]{0:T(512)} %param.15) | copy-start | bytes 4612
  6.5 38.6 %all-gather.5.cloned.1.call-start = ((), (), s32[]{:S(2)}) async-start(), calls=%async_computation.1 | async-start | bytes 3538944 | tf_op jit(solution)/shard_map/all_gather | solution.py:106
  9.5 116.9 %all-gather.7.cloned.1.call-start = ((), (), s32[]{:S(2)}) async-start(), calls=%async_computation.2 | async-start | bytes 5160960 | tf_op jit(solution)/shard_map/all_gather | solution.py:93
  10.3 149.2 %all-gather.9.cloned.1.call-start = ((), (), s32[]{:S(2)}) async-start(), calls=%async_computation.3 | async-start | bytes 3538944 | tf_op jit(solution)/shard_map/all_gather | solution.py:107
  11.3 447.7 %reduce-scatter.2.cloned.1.call-start = ((), (), s32[]{:S(2)}) async-start(), calls=%async_computation.4 | async-start | bytes 5160960 | tf_op jit(solution)/shard_map/reduce_scatter | solution.py:155
  45.2 18.5 %copy-start.1 = (pred[384,3072]{0,1:T(8,128)(4,1)S(1)}, pred[384,3072]{0,1:T(8,128)(4,1)}, u32[]{:S(2)}) copy-start(pred[384,3072]{0,1:T(8,128)(4,1)} %fusion.27) | copy-start | bytes 3538948
  159.5 18.0 %copy-start.7 = (f32[4,2,384]{2,1,0:T(2,128)S(1)}, f32[4,2,384]{2,1,0:T(2,128)}, u32[]{:S(2)}) copy-start(f32[4,2,384]{2,1,0:T(2,128)} %fusion.25) | copy-start | bytes 36868
  159.5 18.0 %copy-start.9 = (f32[4,2,384]{2,1,0:T(2,128)S(1)}, f32[4,2,384]{2,1,0:T(2,128)}, u32[]{:S(2)}) copy-start(f32[4,2,384]{2,1,0:T(2,128)} %copy-done.8) | copy-start | bytes 36868
  179.2 21.9 %collective-permute-start = (bf16[384,512]{0,1:T(8,128)(2,1)S(1)}, bf16[384,512]{0,1:T(8,128)(2,1)}, u32[]{:S(2)}, u32[]{:S(2)}) collective-permute-start(bf16[384,512]{0,1:T(8,128)(2,1)S(1)} %copy.95), channel_id=1, source_target_pairs={{0,4},{4,8},{8,12},{12,16},{16,20},{20,24},{24,28},{28,0},{1,5},{5... | collective-permute-start | bytes 1179656 | tf_op jit(solution)/shard_map/while/body/eval_jaxpr/ppermute | solution.py:17
  179.5 21.6 %collective-permute-start.1 = (bf16[384,512]{1,0:T(8,128)(2,1)S(1)}, bf16[384,512]{1,0:T(8,128)(2,1)S(1)}, u32[]{:S(2)}, u32[]{:S(2)}) collective-permute-start(bf16[384,512]{1,0:T(8,128)(2,1)S(1)} %copy.96), channel_id=1, source_target_pairs={{0,4},{4,8},{8,12},{12,16},{16,20},{20,24},{24,28},{28,0},{1,5},{5... | collective-permute-start | bytes 1179656 | tf_op jit(solution)/shard_map/while/body/eval_jaxpr/ppermute | solution.py:17
  186.8 9.0 %collective-permute-start.2 = (bf16[384,512]{0,1:T(8,128)(2,1)}, bf16[384,512]{0,1:T(8,128)(2,1)}, u32[]{:S(2)}, u32[]{:S(2)}) collective-permute-start(bf16[384,512]{0,1:T(8,128)(2,1)} %fusion.81), channel_id=1, source_target_pairs={{0,4},{4,8},{8,12},{12,16},{16,20},{20,24},{24,28},{28,0},{1,5},{5... | collective-permute-start | bytes 1179656 | tf_op jit(solution)/shard_map/while/body/eval_jaxpr/ppermute | solution.py:17
  188.9 11.1 %collective-permute-start.3 = (bf16[384,512]{0,1:T(8,128)(2,1)}, bf16[384,512]{0,1:T(8,128)(2,1)}, u32[]{:S(2)}, u32[]{:S(2)}) collective-permute-start(bf16[384,512]{0,1:T(8,128)(2,1)} %fusion.83), channel_id=1, source_target_pairs={{0,4},{4,8},{8,12},{12,16},{16,20},{20,24},{24,28},{28,0},{1,5},{5... | collective-permute-start | bytes 1179656 | tf_op jit(solution)/shard_map/while/body/eval_jaxpr/ppermute | solution.py:17
  190.3 10.8 %copy-start.5 = (s32[3072]{0:T(1024)S(1)}, s32[3072]{0:T(1024)}, u32[]{:S(2)}) copy-start(s32[3072]{0:T(1024)} %copy-done.4) | copy-start | bytes 36868 | tf_op jit(solution)/shard_map/while
  202.1 21.9 %collective-permute-start = (bf16[384,512]{0,1:T(8,128)(2,1)S(1)}, bf16[384,512]{0,1:T(8,128)(2,1)}, u32[]{:S(2)}, u32[]{:S(2)}) collective-permute-start(bf16[384,512]{0,1:T(8,128)(2,1)S(1)} %copy.95), channel_id=1, source_target_pairs={{0,4},{4,8},{8,12},{12,16},{16,20},{20,24},{24,28},{28,0},{1,5},{5... | collective-permute-start | bytes 1179656 | tf_op jit(solution)/shard_map/while/body/eval_jaxpr/ppermute | solution.py:17
  202.2 21.9 %collective-permute-start.1 = (bf16[384,512]{1,0:T(8,128)(2,1)S(1)}, bf16[384,512]{1,0:T(8,128)(2,1)S(1)}, u32[]{:S(2)}, u32[]{:S(2)}) collective-permute-start(bf16[384,512]{1,0:T(8,128)(2,1)S(1)} %copy.96), channel_id=1, source_target_pairs={{0,4},{4,8},{8,12},{12,16},{16,20},{20,24},{24,28},{28,0},{1,5},{5... | collective-permute-start | bytes 1179656 | tf_op jit(solution)/shard_map/while/body/eval_jaxpr/ppermute | solution.py:17
  208.8 9.9 %collective-permute-start.2 = (bf16[384,512]{0,1:T(8,128)(2,1)}, bf16[384,512]{0,1:T(8,128)(2,1)}, u32[]{:S(2)}, u32[]{:S(2)}) collective-permute-start(bf16[384,512]{0,1:T(8,128)(2,1)} %fusion.81), channel_id=1, source_target_pairs={{0,4},{4,8},{8,12},{12,16},{16,20},{20,24},{24,28},{28,0},{1,5},{5... | collective-permute-start | bytes 1179656 | tf_op jit(solution)/shard_map/while/body/eval_jaxpr/ppermute | solution.py:17
  210.8 12.2 %collective-permute-start.3 = (bf16[384,512]{0,1:T(8,128)(2,1)}, bf16[384,512]{0,1:T(8,128)(2,1)}, u32[]{:S(2)}, u32[]{:S(2)}) collective-permute-start(bf16[384,512]{0,1:T(8,128)(2,1)} %fusion.83), channel_id=1, source_target_pairs={{0,4},{4,8},{8,12},{12,16},{16,20},{20,24},{24,28},{28,0},{1,5},{5... | collective-permute-start | bytes 1179656 | tf_op jit(solution)/shard_map/while/body/eval_jaxpr/ppermute | solution.py:17
  213.2 10.8 %copy-start.5 = (s32[3072]{0:T(1024)S(1)}, s32[3072]{0:T(1024)}, u32[]{:S(2)}) copy-start(s32[3072]{0:T(1024)} %copy-done.4) | copy-start | bytes 36868 | tf_op jit(solution)/shard_map/while
  225.1 21.9 %collective-permute-start = (bf16[384,512]{0,1:T(8,128)(2,1)S(1)}, bf16[384,512]{0,1:T(8,128)(2,1)}, u32[]{:S(2)}, u32[]{:S(2)}) collective-permute-start(bf16[384,512]{0,1:T(8,128)(2,1)S(1)} %copy.95), channel_id=1, source_target_pairs={{0,4},{4,8},{8,12},{12,16},{16,20},{20,24},{24,28},{28,0},{1,5},{5... | collective-permute-start | bytes 1179656 | tf_op jit(solution)/shard_map/while/body/eval_jaxpr/ppermute | solution.py:17
  225.1 21.9 %collective-permute-start.1 = (bf16[384,512]{1,0:T(8,128)(2,1)S(1)}, bf16[384,512]{1,0:T(8,128)(2,1)S(1)}, u32[]{:S(2)}, u32[]{:S(2)}) collective-permute-start(bf16[384,512]{1,0:T(8,128)(2,1)S(1)} %copy.96), channel_id=1, source_target_pairs={{0,4},{4,8},{8,12},{12,16},{16,20},{20,24},{24,28},{28,0},{1,5},{5... | collective-permute-start | bytes 1179656 | tf_op jit(solution)/shard_map/while/body/eval_jaxpr/ppermute | solution.py:17
  231.2 10.6 %collective-permute-start.2 = (bf16[384,512]{0,1:T(8,128)(2,1)}, bf16[384,512]{0,1:T(8,128)(2,1)}, u32[]{:S(2)}, u32[]{:S(2)}) collective-permute-start(bf16[384,512]{0,1:T(8,128)(2,1)} %fusion.81), channel_id=1, source_target_pairs={{0,4},{4,8},{8,12},{12,16},{16,20},{20,24},{24,28},{28,0},{1,5},{5... | collective-permute-start | bytes 1179656 | tf_op jit(solution)/shard_map/while/body/eval_jaxpr/ppermute | solution.py:17
  233.0 12.9 %collective-permute-start.3 = (bf16[384,512]{0,1:T(8,128)(2,1)}, bf16[384,512]{0,1:T(8,128)(2,1)}, u32[]{:S(2)}, u32[]{:S(2)}) collective-permute-start(bf16[384,512]{0,1:T(8,128)(2,1)} %fusion.83), channel_id=1, source_target_pairs={{0,4},{4,8},{8,12},{12,16},{16,20},{20,24},{24,28},{28,0},{1,5},{5... | collective-permute-start | bytes 1179656 | tf_op jit(solution)/shard_map/while/body/eval_jaxpr/ppermute | solution.py:17
  236.2 10.8 %copy-start.5 = (s32[3072]{0:T(1024)S(1)}, s32[3072]{0:T(1024)}, u32[]{:S(2)}) copy-start(s32[3072]{0:T(1024)} %copy-done.4) | copy-start | bytes 36868 | tf_op jit(solution)/shard_map/while
  248.0 21.9 %collective-permute-start = (bf16[384,512]{0,1:T(8,128)(2,1)S(1)}, bf16[384,512]{0,1:T(8,128)(2,1)}, u32[]{:S(2)}, u32[]{:S(2)}) collective-permute-start(bf16[384,512]{0,1:T(8,128)(2,1)S(1)} %copy.95), channel_id=1, source_target_pairs={{0,4},{4,8},{8,12},{12,16},{16,20},{20,24},{24,28},{28,0},{1,5},{5... | collective-permute-start | bytes 1179656 | tf_op jit(solution)/shard_map/while/body/eval_jaxpr/ppermute | solution.py:17
  248.1 21.9 %collective-permute-start.1 = (bf16[384,512]{1,0:T(8,128)(2,1)S(1)}, bf16[384,512]{1,0:T(8,128)(2,1)S(1)}, u32[]{:S(2)}, u32[]{:S(2)}) collective-permute-start(bf16[384,512]{1,0:T(8,128)(2,1)S(1)} %copy.96), channel_id=1, source_target_pairs={{0,4},{4,8},{8,12},{12,16},{16,20},{20,24},{24,28},{28,0},{1,5},{5... | collective-permute-start | bytes 1179656 | tf_op jit(solution)/shard_map/while/body/eval_jaxpr/ppermute | solution.py:17
  254.1 10.5 %collective-permute-start.2 = (bf16[384,512]{0,1:T(8,128)(2,1)}, bf16[384,512]{0,1:T(8,128)(2,1)}, u32[]{:S(2)}, u32[]{:S(2)}) collective-permute-start(bf16[384,512]{0,1:T(8,128)(2,1)} %fusion.81), channel_id=1, source_target_pairs={{0,4},{4,8},{8,12},{12,16},{16,20},{20,24},{24,28},{28,0},{1,5},{5... | collective-permute-start | bytes 1179656 | tf_op jit(solution)/shard_map/while/body/eval_jaxpr/ppermute | solution.py:17
  256.0 12.9 %collective-permute-start.3 = (bf16[384,512]{0,1:T(8,128)(2,1)}, bf16[384,512]{0,1:T(8,128)(2,1)}, u32[]{:S(2)}, u32[]{:S(2)}) collective-permute-start(bf16[384,512]{0,1:T(8,128)(2,1)} %fusion.83), channel_id=1, source_target_pairs={{0,4},{4,8},{8,12},{12,16},{16,20},{20,24},{24,28},{28,0},{1,5},{5... | collective-permute-start | bytes 1179656 | tf_op jit(solution)/shard_map/while/body/eval_jaxpr/ppermute | solution.py:17
  259.1 10.8 %copy-start.5 = (s32[3072]{0:T(1024)S(1)}, s32[3072]{0:T(1024)}, u32[]{:S(2)}) copy-start(s32[3072]{0:T(1024)} %copy-done.4) | copy-start | bytes 36868 | tf_op jit(solution)/shard_map/while
  271.0 21.9 %collective-permute-start = (bf16[384,512]{0,1:T(8,128)(2,1)S(1)}, bf16[384,512]{0,1:T(8,128)(2,1)}, u32[]{:S(2)}, u32[]{:S(2)}) collective-permute-start(bf16[384,512]{0,1:T(8,128)(2,1)S(1)} %copy.95), channel_id=1, source_target_pairs={{0,4},{4,8},{8,12},{12,16},{16,20},{20,24},{24,28},{28,0},{1,5},{5... | collective-permute-start | bytes 1179656 | tf_op jit(solution)/shard_map/while/body/eval_jaxpr/ppermute | solution.py:17
  271.0 21.9 %collective-permute-start.1 = (bf16[384,512]{1,0:T(8,128)(2,1)S(1)}, bf16[384,512]{1,0:T(8,128)(2,1)S(1)}, u32[]{:S(2)}, u32[]{:S(2)}) collective-permute-start(bf16[384,512]{1,0:T(8,128)(2,1)S(1)} %copy.96), channel_id=1, source_target_pairs={{0,4},{4,8},{8,12},{12,16},{16,20},{20,24},{24,28},{28,0},{1,5},{5... | collective-permute-start | bytes 1179656 | tf_op jit(solution)/shard_map/while/body/eval_jaxpr/ppermute | solution.py:17
  277.1 10.5 %collective-permute-start.2 = (bf16[384,512]{0,1:T(8,128)(2,1)}, bf16[384,512]{0,1:T(8,128)(2,1)}, u32[]{:S(2)}, u32[]{:S(2)}) collective-permute-start(bf16[384,512]{0,1:T(8,128)(2,1)} %fusion.81), channel_id=1, source_target_pairs={{0,4},{4,8},{8,12},{12,16},{16,20},{20,24},{24,28},{28,0},{1,5},{5... | collective-permute-start | bytes 1179656 | tf_op jit(solution)/shard_map/while/body/eval_jaxpr/ppermute | solution.py:17
  278.9 12.9 %collective-permute-start.3 = (bf16[384,512]{0,1:T(8,128)(2,1)}, bf16[384,512]{0,1:T(8,128)(2,1)}, u32[]{:S(2)}, u32[]{:S(2)}) collective-permute-start(bf16[384,512]{0,1:T(8,128)(2,1)} %fusion.83), channel_id=1, source_target_pairs={{0,4},{4,8},{8,12},{12,16},{16,20},{20,24},{24,28},{28,0},{1,5},{5... | collective-permute-start | bytes 1179656 | tf_op jit(solution)/shard_map/while/body/eval_jaxpr/ppermute | solution.py:17
  282.1 10.8 %copy-start.5 = (s32[3072]{0:T(1024)S(1)}, s32[3072]{0:T(1024)}, u32[]{:S(2)}) copy-start(s32[3072]{0:T(1024)} %copy-done.4) | copy-start | bytes 36868 | tf_op jit(solution)/shard_map/while
  293.9 21.9 %collective-permute-start = (bf16[384,512]{0,1:T(8,128)(2,1)S(1)}, bf16[384,512]{0,1:T(8,128)(2,1)}, u32[]{:S(2)}, u32[]{:S(2)}) collective-permute-start(bf16[384,512]{0,1:T(8,128)(2,1)S(1)} %copy.95), channel_id=1, source_target_pairs={{0,4},{4,8},{8,12},{12,16},{16,20},{20,24},{24,28},{28,0},{1,5},{5... | collective-permute-start | bytes 1179656 | tf_op jit(solution)/shard_map/while/body/eval_jaxpr/ppermute | solution.py:17
  294.0 21.9 %collective-permute-start.1 = (bf16[384,512]{1,0:T(8,128)(2,1)S(1)}, bf16[384,512]{1,0:T(8,128)(2,1)S(1)}, u32[]{:S(2)}, u32[]{:S(2)}) collective-permute-start(bf16[384,512]{1,0:T(8,128)(2,1)S(1)} %copy.96), channel_id=1, source_target_pairs={{0,4},{4,8},{8,12},{12,16},{16,20},{20,24},{24,28},{28,0},{1,5},{5... | collective-permute-start | bytes 1179656 | tf_op jit(solution)/shard_map/while/body/eval_jaxpr/ppermute | solution.py:17
  300.0 10.5 %collective-permute-start.2 = (bf16[384,512]{0,1:T(8,128)(2,1)}, bf16[384,512]{0,1:T(8,128)(2,1)}, u32[]{:S(2)}, u32[]{:S(2)}) collective-permute-start(bf16[384,512]{0,1:T(8,128)(2,1)} %fusion.81), channel_id=1, source_target_pairs={{0,4},{4,8},{8,12},{12,16},{16,20},{20,24},{24,28},{28,0},{1,5},{5... | collective-permute-start | bytes 1179656 | tf_op jit(solution)/shard_map/while/body/eval_jaxpr/ppermute | solution.py:17
  301.9 12.9 %collective-permute-start.3 = (bf16[384,512]{0,1:T(8,128)(2,1)}, bf16[384,512]{0,1:T(8,128)(2,1)}, u32[]{:S(2)}, u32[]{:S(2)}) collective-permute-start(bf16[384,512]{0,1:T(8,128)(2,1)} %fusion.83), channel_id=1, source_target_pairs={{0,4},{4,8},{8,12},{12,16},{16,20},{20,24},{24,28},{28,0},{1,5},{5... | collective-permute-start | bytes 1179656 | tf_op jit(solution)/shard_map/while/body/eval_jaxpr/ppermute | solution.py:17
  305.0 10.8 %copy-start.5 = (s32[3072]{0:T(1024)S(1)}, s32[3072]{0:T(1024)}, u32[]{:S(2)}) copy-start(s32[3072]{0:T(1024)} %copy-done.4) | copy-start | bytes 36868 | tf_op jit(solution)/shard_map/while
  316.9 21.9 %collective-permute-start = (bf16[384,512]{0,1:T(8,128)(2,1)S(1)}, bf16[384,512]{0,1:T(8,128)(2,1)}, u32[]{:S(2)}, u32[]{:S(2)}) collective-permute-start(bf16[384,512]{0,1:T(8,128)(2,1)S(1)} %copy.95), channel_id=1, source_target_pairs={{0,4},{4,8},{8,12},{12,16},{16,20},{20,24},{24,28},{28,0},{1,5},{5... | collective-permute-start | bytes 1179656 | tf_op jit(solution)/shard_map/while/body/eval_jaxpr/ppermute | solution.py:17
  316.9 21.9 %collective-permute-start.1 = (bf16[384,512]{1,0:T(8,128)(2,1)S(1)}, bf16[384,512]{1,0:T(8,128)(2,1)S(1)}, u32[]{:S(2)}, u32[]{:S(2)}) collective-permute-start(bf16[384,512]{1,0:T(8,128)(2,1)S(1)} %copy.96), channel_id=1, source_target_pairs={{0,4},{4,8},{8,12},{12,16},{16,20},{20,24},{24,28},{28,0},{1,5},{5... | collective-permute-start | bytes 1179656 | tf_op jit(solution)/shard_map/while/body/eval_jaxpr/ppermute | solution.py:17
  323.0 10.5 %collective-permute-start.2 = (bf16[384,512]{0,1:T(8,128)(2,1)}, bf16[384,512]{0,1:T(8,128)(2,1)}, u32[]{:S(2)}, u32[]{:S(2)}) collective-permute-start(bf16[384,512]{0,1:T(8,128)(2,1)} %fusion.81), channel_id=1, source_target_pairs={{0,4},{4,8},{8,12},{12,16},{16,20},{20,24},{24,28},{28,0},{1,5},{5... | collective-permute-start | bytes 1179656 | tf_op jit(solution)/shard_map/while/body/eval_jaxpr/ppermute | solution.py:17
  324.8 12.9 %collective-permute-start.3 = (bf16[384,512]{0,1:T(8,128)(2,1)}, bf16[384,512]{0,1:T(8,128)(2,1)}, u32[]{:S(2)}, u32[]{:S(2)}) collective-permute-start(bf16[384,512]{0,1:T(8,128)(2,1)} %fusion.83), channel_id=1, source_target_pairs={{0,4},{4,8},{8,12},{12,16},{16,20},{20,24},{24,28},{28,0},{1,5},{5... | collective-permute-start | bytes 1179656 | tf_op jit(solution)/shard_map/while/body/eval_jaxpr/ppermute | solution.py:17
  328.0 10.8 %copy-start.5 = (s32[3072]{0:T(1024)S(1)}, s32[3072]{0:T(1024)}, u32[]{:S(2)}) copy-start(s32[3072]{0:T(1024)} %copy-done.4) | copy-start | bytes 36868 | tf_op jit(solution)/shard_map/while
  339.8 21.9 %collective-permute-start = (bf16[384,512]{0,1:T(8,128)(2,1)S(1)}, bf16[384,512]{0,1:T(8,128)(2,1)}, u32[]{:S(2)}, u32[]{:S(2)}) collective-permute-start(bf16[384,512]{0,1:T(8,128)(2,1)S(1)} %copy.95), channel_id=1, source_target_pairs={{0,4},{4,8},{8,12},{12,16},{16,20},{20,24},{24,28},{28,0},{1,5},{5... | collective-permute-start | bytes 1179656 | tf_op jit(solution)/shard_map/while/body/eval_jaxpr/ppermute | solution.py:17
  339.9 21.9 %collective-permute-start.1 = (bf16[384,512]{1,0:T(8,128)(2,1)S(1)}, bf16[384,512]{1,0:T(8,128)(2,1)S(1)}, u32[]{:S(2)}, u32[]{:S(2)}) collective-permute-start(bf16[384,512]{1,0:T(8,128)(2,1)S(1)} %copy.96), channel_id=1, source_target_pairs={{0,4},{4,8},{8,12},{12,16},{16,20},{20,24},{24,28},{28,0},{1,5},{5... | collective-permute-start | bytes 1179656 | tf_op jit(solution)/shard_map/while/body/eval_jaxpr/ppermute | solution.py:17
  345.9 10.5 %collective-permute-start.2 = (bf16[384,512]{0,1:T(8,128)(2,1)}, bf16[384,512]{0,1:T(8,128)(2,1)}, u32[]{:S(2)}, u32[]{:S(2)}) collective-permute-start(bf16[384,512]{0,1:T(8,128)(2,1)} %fusion.81), channel_id=1, source_target_pairs={{0,4},{4,8},{8,12},{12,16},{16,20},{20,24},{24,28},{28,0},{1,5},{5... | collective-permute-start | bytes 1179656 | tf_op jit(solution)/shard_map/while/body/eval_jaxpr/ppermute | solution.py:17
  347.8 12.9 %collective-permute-start.3 = (bf16[384,512]{0,1:T(8,128)(2,1)}, bf16[384,512]{0,1:T(8,128)(2,1)}, u32[]{:S(2)}, u32[]{:S(2)}) collective-permute-start(bf16[384,512]{0,1:T(8,128)(2,1)} %fusion.83), channel_id=1, source_target_pairs={{0,4},{4,8},{8,12},{12,16},{16,20},{20,24},{24,28},{28,0},{1,5},{5... | collective-permute-start | bytes 1179656 | tf_op jit(solution)/shard_map/while/body/eval_jaxpr/ppermute | solution.py:17
  350.9 10.8 %copy-start.5 = (s32[3072]{0:T(1024)S(1)}, s32[3072]{0:T(1024)}, u32[]{:S(2)}) copy-start(s32[3072]{0:T(1024)} %copy-done.4) | copy-start | bytes 36868 | tf_op jit(solution)/shard_map/while
  (43 other events, 78.4 us)
Sparse Core Ops, SparseCore 0:
  9.7 35.4 all-gather.4
  46.7 79.6 all-gather.6
  128.3 31.2 all-gather.8
  383.8 75.1 reduce-scatter.1
where the time goes:
time: 467 us; the launch traced here: 466 us
  waiting for transfers between devices  209 us (45%)
  matrix products  104 us (22%)
  other arithmetic  74.6 us (16%)
  local copies, waits for them, and re-layouts  30.8 us (7%)
  starting transfers between devices  21.3 us (5%)
  between operations  13.3 us (3%)
  blocking collectives  10.4 us (2%)
    reduce_scatter x1, waiting for transfers between devices, local(): lax.psum_scatter(partial_value.astype(jnp.bfloat16), 'ba', scatter_dimens...  75.3 us
    ppermute x32, waiting for transfers between devices, from_behind(): return lax.ppermute(value, axis, pairs)  47.9 us
    all_gather x1, waiting for transfers between devices, local(): lax.all_gather(grad_out, 'ba', axis=1, tiled=True)  45.9 us
    dot_general x4, matrix products, project_back(): lax.dot_general(grad, weight, (((1,), (1,)), ((), ())), preferred_element...  31.8 us
    dot_general x9, matrix products, block_scores(): jnp.einsum('iagd,jad->agij', dout_four, value_three, preferred_element_ty...  30 us
    dot_general x9, matrix products, block_scores(): jnp.einsum('iagd,jad->agij', query_four, key_three, preferred_element_typ...  23.8 us
    add x8, other arithmetic, step_keys(): return (bundle_next, sums_next, grad_q + add_q)  21.6 us
    ppermute x32, starting transfers between devices, from_behind(): return lax.ppermute(value, axis, pairs)  21.2 us
  transfers between devices with their start and end apart: 36, of which 20 were waited for; matrix products, arithmetic and copies ran while one was open for 34% of the time, Pallas kernels for 0%

commit v1 on v0

--- a/solution.py
+++ b/solution.py
@@ -1,11 +1,16 @@
+import functools
+
 import jax
 import jax.numpy as jnp
 from jax import lax
+from jax.experimental import pallas as pl
+from jax.experimental.pallas import tpu as pltpu
 from jax.sharding import PartitionSpec as P
 
 D = 5376
 HQ = 32
 HD = 128
+DOCS = 6
 
 
 NEG_FILL = -1e30
@@ -83,7 +88,7 @@
     )
 
 
-def local(query, keys, values, grad_out, segment_ids, w_query, w_key, w_value, w_out):
+def local_ring(query, keys, values, grad_out, segment_ids, w_query, w_key, w_value, w_out):
     seq_devices = lax.axis_size("aa")
     own_index = lax.axis_index("aa")
     tok_count = query.shape[0]
@@ -157,6 +162,124 @@
     )
 
 
+def fold_rows(value, op):
+    return op(value.reshape(-1, 8, value.shape[1]), axis=0)
+
+
+def attention_kernel(block, scaling, low_ref, start_ref, qkv_ref, dout_ref, out_ref, s_ref, dp_ref, dk_ref, dv_ref):
+    total = qkv_ref.shape[0]
+    contract_last = (((1,), (1,)), ((), ()))
+    dk_ref[...] = jnp.zeros_like(dk_ref)
+    dv_ref[...] = jnp.zeros_like(dv_ref)
+    lane = lax.broadcasted_iota(jnp.int32, (block, block), 1)
+    sub = lax.broadcasted_iota(jnp.int32, (block, block), 0)
+
+    def query_block(qb, carry):
+        rows = pl.ds(pl.multiple_of(qb * block, block), block)
+        query = qkv_ref[rows, 0:HD]
+        dout = dout_ref[rows, :]
+        low = low_ref[qb]
+        starts = start_ref[pl.ds(qb, 1), :]
+
+        def scores_at(kb, top):
+            cols = pl.ds(pl.multiple_of(kb * block, block), block)
+            s = lax.dot_general(qkv_ref[cols, HD : 2 * HD], query, contract_last, preferred_element_type=jnp.float32)
+            dp = lax.dot_general(qkv_ref[cols, 2 * HD : 3 * HD], dout, contract_last, preferred_element_type=jnp.float32)
+            key_pos = kb * block + sub
+            allowed = (key_pos <= qb * block + lane) & (key_pos >= starts)
+            s = jnp.where(allowed, s * scaling, NEG_FILL)
+            s_ref[cols, :] = s
+            dp_ref[cols, :] = dp
+            return jnp.maximum(top, fold_rows(s, jnp.max))
+
+        top = lax.fori_loop(low, qb + 1, scores_at, jnp.full((8, block), NEG_FILL, jnp.float32))
+        top = jnp.max(top, axis=0, keepdims=True)
+
+        def sums_at(kb, state):
+            run_sum, run_dot = state
+            cols = pl.ds(pl.multiple_of(kb * block, block), block)
+            expo = jnp.exp(s_ref[cols, :] - top)
+            s_ref[cols, :] = expo
+            return (run_sum + fold_rows(expo, jnp.sum), run_dot + fold_rows(expo * dp_ref[cols, :], jnp.sum))
+
+        zero = jnp.zeros((8, block), jnp.float32)
+        run_sum, run_dot = lax.fori_loop(low, qb + 1, sums_at, (zero, zero))
+        inverse = 1.0 / jnp.sum(run_sum, axis=0, keepdims=True)
+        delta = jnp.sum(run_dot, axis=0, keepdims=True) * inverse
+
+        def grads_at(kb, grad_q):
+            cols = pl.ds(pl.multiple_of(kb * block, block), block)
+            probs = s_ref[cols, :] * inverse
+            dscores = (probs * (dp_ref[cols, :] - delta)).astype(jnp.bfloat16)
+            dv_ref[cols, :] += jnp.dot(probs.astype(jnp.bfloat16), dout, preferred_element_type=jnp.float32)
+            dk_ref[cols, :] += jnp.dot(dscores, query, preferred_element_type=jnp.float32)
+            return grad_q + lax.dot_general(
+                dscores, qkv_ref[cols, HD : 2 * HD], (((0,), (0,)), ((), ())), preferred_element_type=jnp.float32
+            )
+
+        grad_q = lax.fori_loop(low, qb + 1, grads_at, jnp.zeros((block, HD), jnp.float32))
+        out_ref[rows, 0:HD] = (grad_q * scaling).astype(jnp.bfloat16)
+        return carry
+
+    lax.fori_loop(0, total // block, query_block, 0)
+    out_ref[:, HD : 2 * HD] = (dk_ref[...] * scaling).astype(jnp.bfloat16)
+    out_ref[:, 2 * HD : 3 * HD] = dv_ref[...].astype(jnp.bfloat16)
+
+
+def one_head(qkv, dout, all_seg, scaling):
+    total = qkv.shape[0]
+    block = 256 if total % 256 == 0 else 128
+    firsts = jnp.sum(all_seg[None, :] < lax.iota(jnp.int32, DOCS)[:, None], axis=1, dtype=jnp.int32)
+    chosen = all_seg[None, :] == lax.iota(jnp.int32, DOCS)[:, None]
+    starts = jnp.sum(jnp.where(chosen, firsts[:, None], 0), axis=0, dtype=jnp.int32).reshape(-1, block)
+    low = starts[:, 0] // block
+    whole = pl.BlockSpec(memory_space=pltpu.VMEM)
+    return pl.pallas_call(
+        functools.partial(attention_kernel, block, scaling),
+        out_shape=jax.ShapeDtypeStruct((total, 3 * HD), jnp.bfloat16),
+        in_specs=[pl.BlockSpec(memory_space=pltpu.SMEM), whole, whole, whole],
+        out_specs=whole,
+        scratch_shapes=[
+            pltpu.VMEM((total, block), jnp.float32),
+            pltpu.VMEM((total, block), jnp.float32),
+            pltpu.VMEM((total, HD), jnp.float32),
+            pltpu.VMEM((total, HD), jnp.float32),
+        ],
+        compiler_params=pltpu.CompilerParams(vmem_limit_bytes=32 * 1024 * 1024),
+        name="attention",
+    )(low, starts, qkv, dout)
+
+
+def local(query, keys, values, grad_out, segment_ids, w_query, w_key, w_value, w_out):
+    seq_devices = lax.axis_size("aa")
+    tok_count = query.shape[0]
+    heads = query.shape[1] // HD
+    groups = keys.shape[1] // HD
+    if heads != seq_devices:
+        return local_ring(query, keys, values, grad_out, segment_ids, w_query, w_key, w_value, w_out)
+    scaling = (D / HQ) ** (-0.5)
+    all_seg = lax.all_gather(segment_ids, "aa", axis=0, tiled=True)
+
+    def by_head(value):
+        return value.reshape(tok_count, -1, HD).transpose(1, 0, 2)
+
+    send = jnp.concatenate(
+        [by_head(query), jnp.repeat(by_head(keys), 2, axis=0), jnp.repeat(by_head(values), 2, axis=0)], axis=2
+    )
+    qkv = lax.all_to_all(send, "aa", 0, 0, tiled=True).reshape(-1, 3 * HD)
+    dout = project_back(lax.all_gather(grad_out, "ba", axis=1, tiled=True), w_out).astype(jnp.bfloat16)
+    dout = lax.all_to_all(by_head(dout), "aa", 0, 0, tiled=True).reshape(-1, HD)
+    grads = one_head(qkv, dout, all_seg, scaling)
+    back = lax.all_to_all(grads.reshape(heads, tok_count, 3 * HD), "aa", 0, 0, tiled=True)
+    grad_q = back[:, :, 0:HD].transpose(1, 0, 2).reshape(tok_count, heads * HD)
+    pairs = back[:, :, HD:].reshape(groups, 2, tok_count, 2 * HD).astype(jnp.float32).sum(axis=1)
+    pairs = pairs.astype(jnp.bfloat16).transpose(1, 0, 2)
+    grad_k = pairs[:, :, 0:HD].reshape(tok_count, groups * HD)
+    grad_v = pairs[:, :, HD:].reshape(tok_count, groups * HD)
+    partial_value = project_back(grad_q, w_query) + project_back(grad_k, w_key) + project_back(grad_v, w_value)
+    return lax.psum_scatter(partial_value.astype(jnp.bfloat16), "ba", scatter_dimension=1, tiled=True)
+
+
 def solution(mesh):
     return jax.shard_map(
         local,

time: 467 us -> 284 us (0.61)
  matrix products: 104 us -> 26.3 us
  other arithmetic: 74.6 us -> 2.24 us
  waiting for transfers between devices: 209 us -> 148 us
  blocking collectives: 10.4 us -> 47.4 us
  Pallas kernels: 0 us -> 30.7 us
  local copies, waits for them, and re-layouts: 30.8 us -> 8.39 us
  starting transfers between devices: 21.3 us -> 8.9 us
    dot_general x42 -> x0, matrix products: 72.6 us -> none  [the longest x9 30 us: block_scores(): jnp.einsum('iagd,jad->agij', dout_four, value_three, preferred_element_ty...]
    ppermute x32 -> x0, waiting for transfers between devices: 47.9 us -> none  [from_behind(): return lax.ppermute(value, axis, pairs)]
    all_gather x2 -> x0, waiting for transfers between devices: 39.5 us -> none  [the longest x1 20.7 us: local(): lax.all_gather(values, 'aa', axis=0, tiled=True)]
    all_to_all x0 -> x1, blocking collectives: none -> 31.9 us  [local(): lax.all_to_all(grads.reshape(heads, tok_count, 3 * HD), 'aa', 0, 0, tiled...]
    pallas_call x0 -> x1, Pallas kernels: none -> 30.7 us  [one_head(): pl.pallas_call(functools.partial(attention_kernel, block, scaling), out_s...]
    convert_element_type x32 -> x0, other arithmetic: 30.5 us -> none  [the longest x8 8.38 us: step_keys(): from_behind((dk_now + add_k).astype(jnp.bfloat16), 'aa', 1)]
    all_gather x1, waiting for transfers between devices: 45.9 us -> 74.4 us  [local(): lax.all_gather(grad_out, 'ba', axis=1, tiled=True)]
    add x25 -> x0, other arithmetic: 22.3 us -> none  [the longest x8 21.6 us: step_keys(): return (bundle_next, sums_next, grad_q + add_q)]
  transfers between devices with their start and end apart: 36 -> 4, of which waited for: 20 -> 2; matrix products, arithmetic and copies ran while one was open for 34% -> 5% of each run, Pallas kernels for 0% -> 0%
where the time goes in v1:
time: 284 us; the launch traced here: 285 us
  waiting for transfers between devices  148 us (52%)
  blocking collectives  47.4 us (17%)
  Pallas kernels  30.7 us (11%)
  matrix products  26.3 us (9%)
  between operations  13.7 us (5%)
  starting transfers between devices  8.9 us (3%)
  local copies, waits for them, and re-layouts  8.39 us (3%)
    all_gather x1, waiting for transfers between devices, local(): lax.all_gather(grad_out, 'ba', axis=1, tiled=True)  74.4 us
    reduce_scatter x1, waiting for transfers between devices, local(): lax.psum_scatter(partial_value.astype(jnp.bfloat16), 'ba', scatter_dimens...  72.6 us
    all_to_all x1, blocking collectives, local(): lax.all_to_all(grads.reshape(heads, tok_count, 3 * HD), 'aa', 0, 0, tiled...  31.9 us
    pallas_call x1, Pallas kernels, one_head(): pl.pallas_call(functools.partial(attention_kernel, block, scaling), out_s...  30.7 us
    dot_general x4, matrix products, project_back(): lax.dot_general(grad, weight, (((1,), (1,)), ((), ())), preferred_element...  26.3 us
    all_gather x1, blocking collectives, local(): all_seg = lax.all_gather(segment_ids, 'aa', axis=0, tiled=True)  15.6 us
  transfers between devices with their start and end apart: 4, of which 2 were waited for; matrix products, arithmetic and copies ran while one was open for 5% of the time, Pallas kernels for 0%

profile of v1, /device:TPU:0, one launch (start us, length us, event | category | flops | bytes accessed | tf_op | source)
XLA Modules:
  0.0 285.3 jit_solution(3192748213500356761)
XLA Ops:
  6.5 0.0 copy-start
  6.5 0.0 all-gather.3.cloned.1.call-start
  6.5 0.7 all-gather.3.cloned.1.call-update
  7.3 1.1 reshape.46
  8.4 0.1 copy.25
  8.4 1.1 reshape.48
  9.5 0.1 copy.26
  9.6 0.0 copy-done
  9.6 0.1 bitcast_bitcast_fusion.1
  9.7 0.1 broadcast_in_dim.25
  9.8 0.1 broadcast_in_dim.26
  10.0 1.8 pad_maximum_fusion
  11.7 5.2 %all-to-all-start = ((bf16[8,384,384]{2,1,0:T(8,128)(2,1)}), bf16[8,384,384]{2,1,0:T(8,128)(2,1)S(1)}, u32[]{:S(2)}, u32[]{:S(2)}) async-start(bf16[8,384,384]{2,1,0:T(8,128)(2,1)} %pad_maximum_fusion), calls=%async_computation | async-start | bytes 4718592 | tf_op jit(solution)/shard_map/all_to_all | solution.py:269
  16.9 74.4 %all-gather.3.cloned.1.call-done = bf16[384,5376]{0,1:T(8,128)(2,1)} async-done(((bf16[384,1344]{0,1:T(8,128)(2,1)}), bf16[384,5376]{0,1:T(8,128)(2,1)}) %all-gather.3.cloned.1.call-update) | async-done | bytes 4128784 | tf_op jit(solution)/shard_map/all_gather | solution.py:270
  91.3 9.9 %fusion.1 = bf16[48,8,8,128]{3,2,1,0:T(8,128)(2,1)S(1)} fusion(bf16[384,5376]{0,1:T(8,128)(2,1)} %all-gather.3.cloned.1.call-done, bf16[1024,5376]{1,0:T(8,128)(2,1)} %param.17), kind=kOutput, calls=%fused_computation.6 | convolution fusion | flops 4228251648 | bytes 15925248 | tf_op jit(solution)/shard_map/dot_general | solution.py:86
  101.2 1.0 copy.33
  102.2 0.0 all-to-all-done
  102.2 3.7 %all-to-all-start.1 = ((bf16[8,384,128]{2,1,0:T(8,128)(2,1)}), bf16[8,384,128]{2,1,0:T(8,128)(2,1)S(1)}, u32[]{:S(2)}, u32[]{:S(2)}) async-start(bf16[8,384,128]{2,1,0:T(8,128)(2,1)} %bitcast.48), calls=%async_computation.1 | async-start | bytes 1572864 | tf_op jit(solution)/shard_map/all_to_all | solution.py:271
  105.9 0.0 reduce-scatter.2.cloned.1.call-start
  105.9 0.0 copy-done.3
  105.9 15.6 %all-gather = s32[8,1,384]{2,1,0:T(1,128)S(1)} all-gather(s32[1,1,384]{2,1,0:T(1,128)S(1)} %reshape.58), channel_id=1, replica_groups=mesh['aa'=8,'ba'=4] {'aa'}, dimensions={0}, use_global_device_ids=true | all-gather | bytes 13824 | tf_op jit(solution)/shard_map/all_gather | solution.py:261
  121.5 0.1 convert_reduce_fusion
  121.7 0.1 select_reduce_fusion
  121.8 0.1 slice_reduce_fusion
  121.9 0.0 all-to-all-done.1
  121.9 30.7 %attention.1 = bf16[3072,384]{1,0:T(8,128)(2,1)S(1)} custom-call(s32[12]{0:T(128)S(1)} %and_select_fusion.low_ref, s32[12,256]{1,0:T(8,128)S(1)} %reshape.44.start_ref, bf16[3072,384]{1,0:T(8,128)(2,1)S(1)} %bitcast.39, bf16[3072,128]{1,0:T(8,128)(2,1)S(1)} %bitcast.41), custom_call_target="tpu_custom_call" | custom-call | tf_op jit(solution)/shard_map/attention/pallas_call | solution.py:237
  152.6 0.0 copy-start.2
  152.6 1.4 copy-done.2
  154.1 3.0 %copy.28 = bf16[8,384,384]{1,2,0:T(8,128)(2,1)S(1)} copy(bf16[8,384,384]{2,1,0:T(8,128)(2,1)} %bitcast.40) | data formatting | bytes 4718592 | tf_op jit(solution)/shard_map/reshape | solution.py:273
  157.1 31.9 %all_to_all.15 = bf16[8,384,384]{1,2,0:T(8,128)(2,1)S(1)} all-to-all(bf16[8,384,384]{1,2,0:T(8,128)(2,1)S(1)} %copy.28), channel_id=1, replica_groups=mesh['aa'=8,'ba'=4] {'aa'}, dimensions={0} | all-to-all | bytes 4718592 | tf_op jit(solution)/shard_map/all_to_all | solution.py:273
  188.9 0.2 bitcast_reduce_fusion
  189.1 0.1 fusion.2
  189.2 0.0 slice-start.2
  189.2 0.1 slice.21
  189.3 0.0 slice-start.3
  189.3 0.0 slice-start
  189.4 8.9 %fusion.3 = f32[384,5376]{0,1:T(8,128)S(1)} fusion(bf16[5376,1024]{1,0:T(8,128)(2,1)} %param.14, bf16[384,1024]{0,1:T(8,128)(2,1)S(1)} %bitcast.54), kind=kOutput, calls=%fused_computation.19 | convolution fusion | flops 4227858432 | bytes 20054016 | tf_op jit(solution)/shard_map/dot_general | solution.py:86
  198.2 0.0 slice-done.2
  198.2 0.0 slice-done.3
  198.3 0.0 slice-start.1
  198.3 3.0 %convolution_add_fusion.1 = f32[384,5376]{0,1:T(8,128)S(1)} fusion(f32[384,5376]{0,1:T(8,128)S(1)} %fusion.3, bf16[5376,512]{1,0:T(8,128)(2,1)S(1)} %bitcast.45, bf16[384,512]{0,1:T(8,128)(2,1)S(1)} %bitcast.50), kind=kOutput, calls=%fused_computation.1 | convolution fusion | flops 2115993600 | bytes 22413312 | tf_op jit(solution)/shard_map/dot_general | solution.py:86
  201.3 0.0 slice-done
  201.3 0.0 slice-done.1
  201.3 0.0 copy-start.1
  201.4 4.6 %fusion = bf16[384,5376]{0,1:T(8,128)(2,1)} fusion(f32[384,5376]{0,1:T(8,128)S(1)} %convolution_add_fusion.1, bf16[5376,512]{1,0:T(8,128)(2,1)S(1)} %bitcast.43, bf16[384,512]{0,1:T(8,128)(2,1)S(1)} %bitcast.53), kind=kOutput, calls=%fused_computation.2 | convolution fusion | flops 2118057984 | bytes 18284544 | tf_op jit(solution)/shard_map/dot_general | solution.py:86
  205.9 0.0 reduce-scatter.2.cloned.1.call-update
  205.9 72.6 %reduce-scatter.2.cloned.1.call-done = bf16[384,1344]{0,1:T(8,128)(2,1)} async-done(((bf16[384,5376]{0,1:T(8,128)(2,1)}), bf16[384,1344]{0,1:T(8,128)(2,1)}) %reduce-scatter.2.cloned.1.call-update) | async-done | bytes 1032208 | tf_op jit(solution)/shard_map/reduce_scatter | solution.py:280
  278.5 0.0 copy-done.1
  (6 shorter events, 0.0 us)
Async XLA Ops:
  6.5 3.0 %copy-start = (bf16[384,1024]{1,0:T(8,128)(2,1)S(1)}, bf16[384,1024]{1,0:T(8,128)(2,1)}, u32[]{:S(2)}) copy-start(bf16[384,1024]{1,0:T(8,128)(2,1)} %param.9) | copy-start | bytes 2359300
  6.5 84.8 %all-gather.3.cloned.1.call-start = ((), (), s32[]{:S(2)}) async-start(), calls=%async_computation.4 | async-start | bytes 5160960 | tf_op jit(solution)/shard_map/all_gather | solution.py:270
  11.7 90.5 %all-to-all-start = ((bf16[8,384,384]{2,1,0:T(8,128)(2,1)}), bf16[8,384,384]{2,1,0:T(8,128)(2,1)S(1)}, u32[]{:S(2)}, u32[]{:S(2)}) async-start(bf16[8,384,384]{2,1,0:T(8,128)(2,1)} %pad_maximum_fusion), calls=%async_computation | async-start | bytes 4718592 | tf_op jit(solution)/shard_map/all_to_all | solution.py:269
  16.9 89.0 %copy-start.3 = (s32[384]{0:T(512)S(1)}, s32[384]{0:T(512)}, u32[]{:S(2)}) copy-start(s32[384]{0:T(512)} %param.13) | copy-start | bytes 4612
  102.2 19.7 %all-to-all-start.1 = ((bf16[8,384,128]{2,1,0:T(8,128)(2,1)}), bf16[8,384,128]{2,1,0:T(8,128)(2,1)S(1)}, u32[]{:S(2)}, u32[]{:S(2)}) async-start(bf16[8,384,128]{2,1,0:T(8,128)(2,1)} %bitcast.48), calls=%async_computation.1 | async-start | bytes 1572864 | tf_op jit(solution)/shard_map/all_to_all | solution.py:271
  105.9 172.6 %reduce-scatter.2.cloned.1.call-start = ((), (), s32[]{:S(2)}) async-start(), calls=%async_computation.5 | async-start | bytes 5160960 | tf_op jit(solution)/shard_map/reduce_scatter | solution.py:280
  152.6 1.4 copy-start.2
  189.2 9.0 %slice-start.2 = ((s8[5505024]{0:T(1024)(128)(4,1)}), s8[4194304]{0:T(1024)(128)(4,1)S(1)}, s32[]{:S(2)}) async-start(s8[5505024]{0:T(1024)(128)(4,1)} %bitcast.44), calls=%async_computation.8 | async-start | bytes 8388608
  189.3 8.9 %slice-start.3 = ((s8[5505024]{0:T(1024)(128)(4,1)}), s8[1310720]{0:T(1024)(128)(4,1)S(1)}, s32[]{:S(2)}) async-start(s8[5505024]{0:T(1024)(128)(4,1)} %bitcast.44), calls=%async_computation.9 | async-start | bytes 2621440
  189.3 12.0 %slice-start = ((s8[5505024]{0:T(1024)(128)(4,1)}), s8[4194304]{0:T(1024)(128)(4,1)S(1)}, s32[]{:S(2)}) async-start(s8[5505024]{0:T(1024)(128)(4,1)} %bitcast.42), calls=%async_computation.6 | async-start | bytes 8388608
  198.3 3.1 %slice-start.1 = ((s8[5505024]{0:T(1024)(128)(4,1)}), s8[1310720]{0:T(1024)(128)(4,1)S(1)}, s32[]{:S(2)}) async-start(s8[5505024]{0:T(1024)(128)(4,1)} %bitcast.42), calls=%async_computation.7 | async-start | bytes 2621440
  201.3 77.2 %copy-start.1 = (bf16[384,1024]{1,0:T(8,128)(2,1)S(1)}, bf16[384,1024]{1,0:T(8,128)(2,1)}, u32[]{:S(2)}) copy-start(bf16[384,1024]{1,0:T(8,128)(2,1)} %param.9) | copy-start | bytes 2359300
Sparse Core Ops, SparseCore 0:
  8.9 82.3 all-gather.2
  206.1 72.3 reduce-scatter.1

commit v2 on v0

--- a/solution.py
+++ b/solution.py
@@ -1,11 +1,16 @@
+import functools
+
 import jax
 import jax.numpy as jnp
 from jax import lax
+from jax.experimental import pallas as pl
+from jax.experimental.pallas import tpu as pltpu
 from jax.sharding import PartitionSpec as P
 
 D = 5376
 HQ = 32
 HD = 128
+DOCS = 6
 
 
 NEG_FILL = -1e30
@@ -83,7 +88,7 @@
     )
 
 
-def local(query, keys, values, grad_out, segment_ids, w_query, w_key, w_value, w_out):
+def local_ring(query, keys, values, grad_out, segment_ids, w_query, w_key, w_value, w_out):
     seq_devices = lax.axis_size("aa")
     own_index = lax.axis_index("aa")
     tok_count = query.shape[0]
@@ -157,6 +162,186 @@
     )
 
 
+def fold_rows(value, op):
+    return op(value.reshape(-1, 8, value.shape[1]), axis=0)
+
+
+CONTRACT_LAST = (((1,), (1,)), ((), ()))
+
+
+def block_of(ref, kb, block, lanes):
+    return ref[pl.ds(pl.multiple_of(kb * block, block), block), lanes]
+
+
+def masked_scores(qkv_ref, query, qb, kb, block, starts, scaling):
+    lane = lax.broadcasted_iota(jnp.int32, (block, block), 1)
+    sub = lax.broadcasted_iota(jnp.int32, (block, block), 0)
+    key = block_of(qkv_ref, kb, block, slice(HD, 2 * HD))
+    s = lax.dot_general(key, query, CONTRACT_LAST, preferred_element_type=jnp.float32)
+    key_pos = kb * block + sub
+    allowed = (key_pos <= qb * block + lane) & (key_pos >= starts)
+    return jnp.where(allowed, s * scaling, NEG_FILL)
+
+
+def stats_kernel(block, scaling, low_ref, start_ref, qkv_ref, lse_ref, s_ref):
+    def query_block(qb, carry):
+        query = block_of(qkv_ref, qb, block, slice(0, HD))
+        low = low_ref[qb]
+        starts = start_ref[pl.ds(qb, 1), :]
+
+        def scores_at(kb, top):
+            s = masked_scores(qkv_ref, query, qb, kb, block, starts, scaling)
+            s_ref[pl.ds(pl.multiple_of(kb * block, block), block), :] = s
+            return jnp.maximum(top, fold_rows(s, jnp.max))
+
+        top = lax.fori_loop(low, qb + 1, scores_at, jnp.full((8, block), NEG_FILL, jnp.float32))
+        top = jnp.max(top, axis=0, keepdims=True)
+
+        def sums_at(kb, run_sum):
+            return run_sum + fold_rows(jnp.exp(block_of(s_ref, kb, block, slice(None)) - top), jnp.sum)
+
+        run_sum = lax.fori_loop(low, qb + 1, sums_at, jnp.zeros((8, block), jnp.float32))
+        lse_ref[pl.ds(qb, 1), :] = top + jnp.log(jnp.sum(run_sum, axis=0, keepdims=True))
+        return carry
+
+    lax.fori_loop(0, qkv_ref.shape[0] // block, query_block, 0)
+
+
+def grads_kernel(block, scaling, low_ref, start_ref, lse_ref, qkv_ref, dout_ref, gq_ref, gkv_ref, p_ref, dp_ref, dk_ref, dv_ref):
+    dk_ref[...] = jnp.zeros_like(dk_ref)
+    dv_ref[...] = jnp.zeros_like(dv_ref)
+
+    def query_block(qb, carry):
+        rows = pl.ds(pl.multiple_of(qb * block, block), block)
+        query = qkv_ref[rows, 0:HD]
+        dout = dout_ref[rows, :]
+        low = low_ref[qb]
+        starts = start_ref[pl.ds(qb, 1), :]
+        lse = lse_ref[pl.ds(qb, 1), :]
+
+        def probs_at(kb, run_dot):
+            cols = pl.ds(pl.multiple_of(kb * block, block), block)
+            s = masked_scores(qkv_ref, query, qb, kb, block, starts, scaling)
+            value = qkv_ref[cols, 2 * HD : 3 * HD]
+            dp = lax.dot_general(value, dout, CONTRACT_LAST, preferred_element_type=jnp.float32)
+            probs = jnp.exp(s - lse)
+            p_ref[cols, :] = probs
+            dp_ref[cols, :] = dp
+            return run_dot + fold_rows(probs * dp, jnp.sum)
+
+        run_dot = lax.fori_loop(low, qb + 1, probs_at, jnp.zeros((8, block), jnp.float32))
+        delta = jnp.sum(run_dot, axis=0, keepdims=True)
+
+        def grads_at(kb, grad_q):
+            cols = pl.ds(pl.multiple_of(kb * block, block), block)
+            probs = p_ref[cols, :]
+            dscores = (probs * (dp_ref[cols, :] - delta)).astype(jnp.bfloat16)
+            dv_ref[cols, :] += jnp.dot(probs.astype(jnp.bfloat16), dout, preferred_element_type=jnp.float32)
+            dk_ref[cols, :] += jnp.dot(dscores, query, preferred_element_type=jnp.float32)
+            return grad_q + lax.dot_general(
+                dscores, qkv_ref[cols, HD : 2 * HD], (((0,), (0,)), ((), ())), preferred_element_type=jnp.float32
+            )
+
+        grad_q = lax.fori_loop(low, qb + 1, grads_at, jnp.zeros((block, HD), jnp.float32))
+        gq_ref[rows, :] = (grad_q * scaling).astype(jnp.bfloat16)
+        return carry
+
+    lax.fori_loop(0, qkv_ref.shape[0] // block, query_block, 0)
+    gkv_ref[:, 0:HD] = (dk_ref[...] * scaling).astype(jnp.bfloat16)
+    gkv_ref[:, HD : 2 * HD] = dv_ref[...].astype(jnp.bfloat16)
+
+
+def document_starts(all_seg, block):
+    chosen = all_seg[None, :] == lax.iota(jnp.int32, DOCS)[:, None]
+    firsts = jnp.sum(all_seg[None, :] < lax.iota(jnp.int32, DOCS)[:, None], axis=1, dtype=jnp.int32)
+    starts = jnp.sum(jnp.where(chosen, firsts[:, None], 0), axis=0, dtype=jnp.int32).reshape(-1, block)
+    return starts[:, 0] // block, starts
+
+
+WHOLE = pl.BlockSpec(memory_space=pltpu.VMEM)
+SCALARS = pl.BlockSpec(memory_space=pltpu.SMEM)
+
+
+def head_stats(low, starts, qkv, scaling):
+    total, block = qkv.shape[0], starts.shape[1]
+    return pl.pallas_call(
+        functools.partial(stats_kernel, block, scaling),
+        out_shape=jax.ShapeDtypeStruct(starts.shape, jnp.float32),
+        in_specs=[SCALARS, WHOLE, WHOLE],
+        out_specs=WHOLE,
+        scratch_shapes=[pltpu.VMEM((total, block), jnp.float32)],
+        compiler_params=pltpu.CompilerParams(vmem_limit_bytes=16 * 1024 * 1024),
+        cost_estimate=pl.CostEstimate(flops=total * total * HD, bytes_accessed=qkv.size * 2, transcendentals=total * total // 2),
+        name="stats",
+    )(low, starts, qkv)
+
+
+def head_grads(low, starts, lse, qkv, dout, scaling):
+    total, block = qkv.shape[0], starts.shape[1]
+    return pl.pallas_call(
+        functools.partial(grads_kernel, block, scaling),
+        out_shape=[
+            jax.ShapeDtypeStruct((total, HD), jnp.bfloat16),
+            jax.ShapeDtypeStruct((total, 2 * HD), jnp.bfloat16),
+        ],
+        in_specs=[SCALARS, WHOLE, WHOLE, WHOLE, WHOLE],
+        out_specs=[WHOLE, WHOLE],
+        scratch_shapes=[
+            pltpu.VMEM((total, block), jnp.float32),
+            pltpu.VMEM((total, block), jnp.float32),
+            pltpu.VMEM((total, HD), jnp.float32),
+            pltpu.VMEM((total, HD), jnp.float32),
+        ],
+        compiler_params=pltpu.CompilerParams(vmem_limit_bytes=32 * 1024 * 1024),
+        cost_estimate=pl.CostEstimate(flops=5 * total * total * HD, bytes_accessed=qkv.size * 6, transcendentals=total * total // 2),
+        name="grads",
+    )(low, starts, lse, qkv, dout)
+
+
+def local(query, keys, values, grad_out, segment_ids, w_query, w_key, w_value, w_out):
+    seq_devices = lax.axis_size("aa")
+    tok_count = query.shape[0]
+    heads = query.shape[1] // HD
+    groups = keys.shape[1] // HD
+    if heads != seq_devices:
+        return local_ring(query, keys, values, grad_out, segment_ids, w_query, w_key, w_value, w_out)
+    scaling = (D / HQ) ** (-0.5)
+    block = 256 if (tok_count * seq_devices) % 256 == 0 else 128
+
+    def by_head(value):
+        return value.reshape(value.shape[0], -1, HD).transpose(1, 0, 2)
+
+    def exchange(value):
+        return lax.all_to_all(value, "aa", 0, 0, tiled=True)
+
+    gathered = lax.all_gather(grad_out, "ba", axis=1, tiled=True)
+    all_seg = lax.all_gather(segment_ids, "aa", axis=0, tiled=True)
+    low, starts = document_starts(all_seg, block)
+    send = jnp.concatenate(
+        [by_head(query), jnp.repeat(by_head(keys), 2, axis=0), jnp.repeat(by_head(values), 2, axis=0)], axis=2
+    )
+    qkv = exchange(send).reshape(-1, 3 * HD)
+    lse = head_stats(low, starts, qkv, scaling)
+    gathered, lse = lax.optimization_barrier((gathered, lse))
+    dout = exchange(by_head(project_back(gathered, w_out).astype(jnp.bfloat16))).reshape(-1, HD)
+    grad_q, grad_kv = head_grads(low, starts, lse, qkv, dout, scaling)
+    half = tok_count // 2
+    odd = lax.axis_index("aa") % 2
+    grad_kv = grad_kv.reshape(heads, 2, half, 2 * HD)
+    own = lax.dynamic_index_in_dim(grad_kv, odd, 1, keepdims=False)
+    other = lax.dynamic_index_in_dim(grad_kv, 1 - odd, 1, keepdims=False)
+    other = lax.ppermute(other, "aa", [(source, source ^ 1) for source in range(seq_devices)])
+    back_q = exchange(grad_q.reshape(heads, tok_count, HD))
+    own = (own.astype(jnp.float32) + other.astype(jnp.float32)).astype(jnp.bfloat16)
+    back_q, own = lax.optimization_barrier((back_q, own))
+    back_kv = exchange(own).reshape(groups, 2 * half, 2 * HD).transpose(1, 0, 2)
+    grad_q = back_q.transpose(1, 0, 2).reshape(tok_count, heads * HD)
+    grad_k = back_kv[:, :, 0:HD].reshape(tok_count, groups * HD)
+    grad_v = back_kv[:, :, HD:].reshape(tok_count, groups * HD)
+    part = project_back(grad_q, w_query) + project_back(grad_k, w_key) + project_back(grad_v, w_value)
+    return lax.psum_scatter(part.astype(jnp.bfloat16), "ba", scatter_dimension=1, tiled=True)
+
+
 def solution(mesh):
     return jax.shard_map(
         local,

time: 467 us -> 274 us (0.59)
  waiting for transfers between devices: 209 us -> 127 us
  matrix products: 104 us -> 33.5 us
  other arithmetic: 74.6 us -> 4.24 us
  Pallas kernels: 0 us -> 39.3 us
  local copies, waits for them, and re-layouts: 30.8 us -> 8.06 us
  blocking collectives: 10.4 us -> 32.5 us
  starting transfers between devices: 21.3 us -> 16.2 us
    dot_general x42 -> x0, matrix products: 72.6 us -> none  [the longest x9 30 us: block_scores(): jnp.einsum('iagd,jad->agij', dout_four, value_three, preferred_element_ty...]
    all_gather x3 -> x1, waiting for transfers between devices: 85.5 us -> 28.7 us  [local(): gathered = lax.all_gather(grad_out, 'ba', axis=1, tiled=True)]
    ppermute x32 -> x1, waiting for transfers between devices: 47.9 us -> 0.01 us  [local(): lax.ppermute(other, 'aa', [(source, source ^ 1) for source in range(seq_d...]
    pallas_call x0 -> x2, Pallas kernels: none -> 39.3 us  [the longest x1 26.5 us: head_grads(): pl.pallas_call(functools.partial(grads_kernel, block, scaling), out_shape...]
    convert_element_type x32 -> x1, other arithmetic: 30.5 us -> 2.21 us  [local(): (own.astype(jnp.float32) + other.astype(jnp.float32)).astype(jnp.bfloat16)]
    all_to_all x0 -> x4, waiting for transfers between devices: none -> 24.5 us  [exchange(): return lax.all_to_all(value, 'aa', 0, 0, tiled=True)]
    add x25 -> x0, other arithmetic: 22.3 us -> none  [the longest x8 21.6 us: step_keys(): return (bundle_next, sums_next, grad_q + add_q)]
    all_gather x1, blocking collectives: 10.4 us -> 32.5 us  [local(): all_seg = lax.all_gather(segment_ids, 'aa', axis=0, tiled=True)]
  transfers between devices with their start and end apart: 36 -> 7, of which waited for: 20 -> 5; matrix products, arithmetic and copies ran while one was open for 34% -> 7% of each run, Pallas kernels for 0% -> 5%
where the time goes in v2:
time: 274 us
  waiting for transfers between devices  127 us (46%)
  Pallas kernels  39.3 us (14%)
  matrix products  33.5 us (12%)
  blocking collectives  32.5 us (12%)
  starting transfers between devices  16.2 us (6%)
  between operations  13.6 us (5%)
  local copies, waits for them, and re-layouts  8.06 us (3%)
  other arithmetic  4.24 us (2%)
    reduce_scatter x1, waiting for transfers between devices, local(): lax.psum_scatter(part.astype(jnp.bfloat16), 'ba', scatter_dimension=1, ti...  73 us
    dot_general x4, matrix products, project_back(): lax.dot_general(grad, weight, (((1,), (1,)), ((), ())), preferred_element...  33.5 us
    all_gather x1, blocking collectives, local(): all_seg = lax.all_gather(segment_ids, 'aa', axis=0, tiled=True)  32.5 us
    all_gather x1, waiting for transfers between devices, local(): gathered = lax.all_gather(grad_out, 'ba', axis=1, tiled=True)  28.7 us
    pallas_call x1, Pallas kernels, head_grads(): pl.pallas_call(functools.partial(grads_kernel, block, scaling), out_shape...  26.5 us
    all_to_all x4, waiting for transfers between devices, exchange(): return lax.all_to_all(value, 'aa', 0, 0, tiled=True)  24.5 us
    all_to_all x4, starting transfers between devices, exchange(): return lax.all_to_all(value, 'aa', 0, 0, tiled=True)  15.9 us
    pallas_call x1, Pallas kernels, head_stats(): pl.pallas_call(functools.partial(stats_kernel, block, scaling), out_shape...  12.8 us
  transfers between devices with their start and end apart: 7, of which 5 were waited for; matrix products, arithmetic and copies ran while one was open for 7% of the time, Pallas kernels for 5%

profile of v2, /device:TPU:0, one launch (start us, length us, event | category | flops | bytes accessed | tf_op | source)
XLA Modules:
  0.0 274.3 jit_solution(5292813268666439086)
XLA Ops:
  6.5 0.0 copy-start
  6.5 0.7 all-gather.3.cloned.1.call-update
  7.3 1.1 reshape.51
  8.4 0.1 copy.36
  8.4 1.1 reshape.53
  9.5 0.1 copy.37
  9.6 0.1 bitcast_bitcast_fusion.1
  9.7 0.1 broadcast_in_dim.25
  9.8 0.0 copy-start.4
  9.9 0.1 broadcast_in_dim.26
  10.0 1.8 pad_maximum_fusion
  11.7 5.2 %all-to-all-start = ((bf16[8,384,384]{2,1,0:T(8,128)(2,1)}), bf16[8,384,384]{2,1,0:T(8,128)(2,1)S(1)}, u32[]{:S(2)}, u32[]{:S(2)}) async-start(bf16[8,384,384]{2,1,0:T(8,128)(2,1)} %pad_maximum_fusion), calls=%async_computation | async-start | bytes 4718592 | tf_op jit(solution)/shard_map/all_to_all | solution.py:315
  17.0 32.5 %all-gather = s32[8,1,384]{2,1,0:T(1,128)S(1)} all-gather(s32[1,1,384]{2,1,0:T(1,128)S(1)} %reshape.65), channel_id=1, replica_groups=mesh['aa'=8,'ba'=4] {'aa'}, dimensions={0}, use_global_device_ids=true | all-gather | bytes 13824 | tf_op jit(solution)/shard_map/all_gather | solution.py:318
  49.4 0.1 convert_reduce_fusion
  49.6 0.1 select_reduce_fusion
  49.7 0.1 slice_reduce_fusion
  49.8 0.0 all-to-all-done
  49.8 12.8 %stats.1.lse_ref = f32[12,256]{1,0:T(8,128)S(1)} custom-call(s32[12]{0:T(128)S(1)} %and_select_fusion.low_ref, s32[12,256]{1,0:T(8,128)S(1)} %reshape.49.start_ref, bf16[3072,384]{1,0:T(8,128)(2,1)S(1)} %bitcast.47), custom_call_target="tpu_custom_call" | custom-call | flops 1207959552 | bytes 2359296 | tf_op jit(solution)/shard_map/stats/pallas_call | solution.py:267
  62.7 28.7 %all-gather.3.cloned.1.call-done = bf16[384,5376]{0,1:T(8,128)(2,1)} async-done(((bf16[384,1344]{0,1:T(8,128)(2,1)}), bf16[384,5376]{0,1:T(8,128)(2,1)}) %all-gather.3.cloned.1.call-update) | async-done | bytes 4128784 | tf_op jit(solution)/shard_map/all_gather | solution.py:317
  91.3 9.9 %fusion.2 = bf16[48,8,8,128]{3,2,1,0:T(8,128)(2,1)S(1)} fusion(bf16[384,5376]{0,1:T(8,128)(2,1)} %all-gather.3.cloned.1.call-done, bf16[1024,5376]{1,0:T(8,128)(2,1)} %param.17), kind=kOutput, calls=%fused_computation.7 | convolution fusion | flops 4228251648 | bytes 15925248 | tf_op jit(solution)/shard_map/dot_general | solution.py:86
  101.2 1.0 copy.48
  102.2 3.7 %all-to-all-start.1 = ((bf16[8,384,128]{2,1,0:T(8,128)(2,1)}), bf16[8,384,128]{2,1,0:T(8,128)(2,1)S(1)}, u32[]{:S(2)}, u32[]{:S(2)}) async-start(bf16[8,384,128]{2,1,0:T(8,128)(2,1)} %bitcast.57), calls=%async_computation.1 | async-start | bytes 1572864 | tf_op jit(solution)/shard_map/all_to_all | solution.py:315
  105.9 12.6 %all-to-all-done.1 = bf16[8,384,128]{2,1,0:T(8,128)(2,1)S(1)} async-done(((bf16[8,384,128]{2,1,0:T(8,128)(2,1)}), bf16[8,384,128]{2,1,0:T(8,128)(2,1)S(1)}, u32[]{:S(2)}, u32[]{:S(2)}) %all-to-all-start.1) | async-done | bytes 786464 | tf_op jit(solution)/shard_map/all_to_all | solution.py:315
  118.4 26.5 %grads.1 = (bf16[3072,128]{1,0:T(8,128)(2,1)S(1)}, bf16[3072,256]{1,0:T(8,128)(2,1)S(1)}) custom-call(s32[12]{0:T(128)S(1)} %and_select_fusion.low_ref, s32[12,256]{1,0:T(8,128)S(1)} %reshape.49.start_ref, f32[12,256]{1,0:T(8,128)S(1)} %stats.1.lse_ref, bf16[3072,384]{1,0:T(8,128)(2,1)S(1)} %bitcast.48, bf16[3072,128]{1,0:T(8,128)(2,1)S(1)} %bitcast.51), custom_call_target="tpu_custom_call" | custom-call | flops 6039797760 | bytes 7077888 | tf_op jit(solution)/shard_map/grads/pallas_call | solution.py:281
  144.9 0.0 copy-start.3
  144.9 1.1 copy-done.2
  146.1 0.1 dynamic-slice_bitcast_fusion
  146.1 0.2 copy-done.3
  146.3 0.0 collective-permute-start
  146.3 2.3 copy.39
  148.6 3.5 %all-to-all-start.2 = ((bf16[8,384,128]{1,2,0:T(8,128)(2,1)}), bf16[8,384,128]{1,2,0:T(8,128)(2,1)S(1)}, u32[]{:S(2)}, u32[]{:S(2)}) async-start(bf16[8,384,128]{1,2,0:T(8,128)(2,1)} %copy.39), calls=%async_computation.2 | async-start | bytes 1572864 | tf_op jit(solution)/shard_map/all_to_all | solution.py:315
  152.2 0.0 collective-permute-done
  152.2 2.2 fusion.1
  154.4 10.3 %all-to-all-done.2 = bf16[8,384,128]{1,2,0:T(8,128)(2,1)S(1)} async-done(((bf16[8,384,128]{1,2,0:T(8,128)(2,1)}), bf16[8,384,128]{1,2,0:T(8,128)(2,1)S(1)}, u32[]{:S(2)}, u32[]{:S(2)}) %all-to-all-start.2) | async-done | bytes 786464 | tf_op jit(solution)/shard_map/all_to_all | solution.py:315
  164.7 3.5 %all-to-all-start.3 = ((bf16[8,192,256]{2,1,0:T(8,128)(2,1)}), bf16[8,192,256]{2,1,0:T(8,128)(2,1)S(1)}, u32[]{:S(2)}, u32[]{:S(2)}) async-start(bf16[8,192,256]{2,1,0:T(8,128)(2,1)} %fusion.1), calls=%async_computation.3 | async-start | bytes 1572864 | tf_op jit(solution)/shard_map/all_to_all | solution.py:315
  168.2 0.2 reduce-scatter.2.cloned.1.call-start
  168.4 10.6 %fusion.4 = f32[384,5376]{0,1:T(8,128)} fusion(bf16[5376,1024]{1,0:T(8,128)(2,1)} %param.14, bf16[384,1024]{0,1:T(8,128)(2,1)S(1)} %bitcast.63), kind=kOutput, calls=%fused_computation.21 | convolution fusion | flops 4227858432 | bytes 20054016 | tf_op jit(solution)/shard_map/dot_general | solution.py:86
  179.0 1.7 all-to-all-done.3
  180.7 0.1 fusion.3
  180.9 0.0 slice-start
  180.9 0.2 copy.42
  181.1 0.2 copy.41
  181.3 0.0 slice-start.1
  181.3 8.4 %convolution_add_fusion.1 = f32[384,5376]{0,1:T(8,128)S(1)} fusion(f32[384,5376]{0,1:T(8,128)} %fusion.4, bf16[5376,512]{1,0:T(8,128)(2,1)} %param.15, bf16[384,512]{0,1:T(8,128)(2,1)S(1)} %bitcast.59), kind=kOutput, calls=%fused_computation.1 | convolution fusion | flops 2115993600 | bytes 22413312 | tf_op jit(solution)/shard_map/dot_general | solution.py:86
  189.8 0.0 copy-start.1
  189.8 4.7 %fusion = bf16[384,5376]{0,1:T(8,128)(2,1)} fusion(f32[384,5376]{0,1:T(8,128)S(1)} %convolution_add_fusion.1, bf16[5376,512]{1,0:T(8,128)(2,1)S(1)} %bitcast.54, bf16[384,512]{0,1:T(8,128)(2,1)S(1)} %bitcast.62), kind=kOutput, calls=%fused_computation.2 | convolution fusion | flops 2118057984 | bytes 18284544 | tf_op jit(solution)/shard_map/dot_general | solution.py:86
  194.5 0.0 reduce-scatter.2.cloned.1.call-update
  194.5 73.0 %reduce-scatter.2.cloned.1.call-done = bf16[384,1344]{0,1:T(8,128)(2,1)} async-done(((bf16[384,5376]{0,1:T(8,128)(2,1)}), bf16[384,1344]{0,1:T(8,128)(2,1)}) %reduce-scatter.2.cloned.1.call-update) | async-done | bytes 1032208 | tf_op jit(solution)/shard_map/reduce_scatter | solution.py:342
  (11 shorter events, 0.0 us)
Async XLA Ops:
  6.5 3.0 %copy-start = (bf16[384,1024]{1,0:T(8,128)(2,1)S(1)}, bf16[384,1024]{1,0:T(8,128)(2,1)}, u32[]{:S(2)}) copy-start(bf16[384,1024]{1,0:T(8,128)(2,1)} %param.9) | copy-start | bytes 2359300
  6.5 84.8 %all-gather.3.cloned.1.call-start = ((), (), s32[]{:S(2)}) async-start(), calls=%async_computation.5 | async-start | bytes 5160960 | tf_op jit(solution)/shard_map/all_gather | solution.py:317
  9.8 7.1 %copy-start.4 = (s32[384]{0:T(512)S(1)}, s32[384]{0:T(512)}, u32[]{:S(2)}) copy-start(s32[384]{0:T(512)} %param.13) | copy-start | bytes 4612
  11.7 38.1 %all-to-all-start = ((bf16[8,384,384]{2,1,0:T(8,128)(2,1)}), bf16[8,384,384]{2,1,0:T(8,128)(2,1)S(1)}, u32[]{:S(2)}, u32[]{:S(2)}) async-start(bf16[8,384,384]{2,1,0:T(8,128)(2,1)} %pad_maximum_fusion), calls=%async_computation | async-start | bytes 4718592 | tf_op jit(solution)/shard_map/all_to_all | solution.py:315
  102.2 16.2 %all-to-all-start.1 = ((bf16[8,384,128]{2,1,0:T(8,128)(2,1)}), bf16[8,384,128]{2,1,0:T(8,128)(2,1)S(1)}, u32[]{:S(2)}, u32[]{:S(2)}) async-start(bf16[8,384,128]{2,1,0:T(8,128)(2,1)} %bitcast.57), calls=%async_computation.1 | async-start | bytes 1572864 | tf_op jit(solution)/shard_map/all_to_all | solution.py:315
  144.9 1.2 copy-start.2
  144.9 1.4 copy-start.3
  146.3 5.9 %collective-permute-start = (bf16[8,192,256]{2,1,0:T(8,128)(2,1)S(1)}, bf16[8,192,256]{2,1,0:T(8,128)(2,1)S(1)}, u32[]{:S(2)}, u32[]{:S(2)}) collective-permute-start(bf16[8,192,256]{2,1,0:T(8,128)(2,1)S(1)} %dynamic-slice_bitcast_fusion), channel_id=1, source_target_pairs={{0,4},{4,0},{8,12},{12,8},{16,20},{20,16},{24,28},{28,24},{1,5},{5... | collective-permute-start | bytes 2359304 | tf_op jit(solution)/shard_map/ppermute | solution.py:333
  148.6 16.1 %all-to-all-start.2 = ((bf16[8,384,128]{1,2,0:T(8,128)(2,1)}), bf16[8,384,128]{1,2,0:T(8,128)(2,1)S(1)}, u32[]{:S(2)}, u32[]{:S(2)}) async-start(bf16[8,384,128]{1,2,0:T(8,128)(2,1)} %copy.39), calls=%async_computation.2 | async-start | bytes 1572864 | tf_op jit(solution)/shard_map/all_to_all | solution.py:315
  164.7 16.1 %all-to-all-start.3 = ((bf16[8,192,256]{2,1,0:T(8,128)(2,1)}), bf16[8,192,256]{2,1,0:T(8,128)(2,1)S(1)}, u32[]{:S(2)}, u32[]{:S(2)}) async-start(bf16[8,192,256]{2,1,0:T(8,128)(2,1)} %fusion.1), calls=%async_computation.3 | async-start | bytes 1572864 | tf_op jit(solution)/shard_map/all_to_all | solution.py:315
  168.2 99.2 %reduce-scatter.2.cloned.1.call-start = ((), (), s32[]{:S(2)}) async-start(), calls=%async_computation.6 | async-start | bytes 5160960 | tf_op jit(solution)/shard_map/reduce_scatter | solution.py:342
  180.9 8.9 %slice-start = ((s8[5505024]{0:T(1024)(128)(4,1)}), s8[1310720]{0:T(1024)(128)(4,1)S(1)}, s32[]{:S(2)}) async-start(s8[5505024]{0:T(1024)(128)(4,1)} %bitcast.53), calls=%async_computation.7 | async-start | bytes 2621440
  181.3 8.4 %slice-start.1 = ((s8[5505024]{0:T(1024)(128)(4,1)}), s8[4194304]{0:T(1024)(128)(4,1)S(1)}, s32[]{:S(2)}) async-start(s8[5505024]{0:T(1024)(128)(4,1)} %bitcast.53), calls=%async_computation.8 | async-start | bytes 8388608
  189.8 77.7 %copy-start.1 = (bf16[384,1024]{1,0:T(8,128)(2,1)S(1)}, bf16[384,1024]{1,0:T(8,128)(2,1)}, u32[]{:S(2)}) copy-start(bf16[384,1024]{1,0:T(8,128)(2,1)} %param.9) | copy-start | bytes 2359300
Sparse Core Ops, SparseCore 0:
  8.9 82.3 all-gather.2
  194.6 72.7 reduce-scatter.1
